TPU v7x, 32 devices: a whole 2x2x4 slice. The times are simulated.
32 devices in a mesh: pb: 4 (over y, core), pa: 8 (over z, x).
Axes of the slice: x: 2, y: 2, z: 4, core: 2. Of those that a mesh axis runs over, the one named last changes fastest.
Arguments:
- query_hidden: bfloat16 [32, 32, 2048], P('pb', 'pa'), may hold values from -32 to 32
- page_hidden: bfloat16 [8, 1024, 2048], P('pa', 'pb'), may hold values from -4.2 to 4.2
- projection: bfloat16 [2048, 128], replicated, may hold values from -0.125 to 0.125
- clicks: int32 [32, 8, 2], P('pb'), may hold values from 0 to 7, as said below
- bins: int32 [32, 8], P('pb'), may hold values from 0 to 7
Outputs:
- query_grad: bfloat16 [32, 32, 2048], P('pb', 'pa')
- page_grad: bfloat16 [8, 1024, 2048], P('pa', 'pb')
- weight_grad: float32 [2048, 128], P(('pb', 'pa'))
Inputs may be any that keep to these rules, and one draw needn't show every extreme that they name: `clicks`: the two pages of a pair always differ.
All inputs are finite; a program needn't handle non-finite values.
Results may differ from a plain program's by a relative error of at most 0.019.
Values may be sent and summed in bfloat16 or wider, within the bound.
A program may use at most 64 MiB of HBM per device.

v0:
```python
import functools

import jax
import jax.numpy as jnp
from jax import lax
from jax.experimental import pallas as pl
from jax.experimental.pallas import tpu as pltpu
from jax.sharding import PartitionSpec as P

sharpness = 0.25
MESH = pl.DeviceIdType.MESH
BF = jnp.bfloat16
F32 = jnp.float32


def dot(x, y, dims):
    return lax.dot_general(x, y, (dims, ((), ())), preferred_element_type=F32)


def kernel(
    PB, PA, qh_hbm, ph_hbm, proj_hbm, clicks_hbm, bins_hbm,
    qg_ref, pg_ref, w_ref,
    clicks_ref, bins_ref, qraw, qh, ph, pht, proj, qe, pe, ebuf, pbuf, sc, gsend, grecv, tsend, trecv,
    wq, w1send, w1recv, w2send, w2recv,
    ls, qs, qr, ps, pr, ss, sr, gs, gr, ts, tr, us, ur, vs, vr,
):
    b = lax.axis_index("pb")
    a = lax.axis_index("pa")
    queries, token_local, hidden = qh_hbm.shape
    rows = queries * token_local
    E = proj.shape[1]
    tokens = PA * rows
    half = PB // 2
    parity = lax.rem(b, 2)
    level = b // 2

    def remote(src, dst, send, recv, to_b, to_a):
        return pltpu.make_async_remote_copy(
            src_ref=src, dst_ref=dst, send_sem=send, recv_sem=recv,
            device_id=(to_b, to_a), device_id_type=MESH,
        )

    loads = [
        pltpu.make_async_copy(qh_hbm, qraw, ls.at[0]),
        pltpu.make_async_copy(proj_hbm, proj, ls.at[1]),
        pltpu.make_async_copy(ph_hbm, ph, ls.at[2]),
        pltpu.make_async_copy(clicks_hbm, clicks_ref, ls.at[3]),
        pltpu.make_async_copy(bins_hbm, bins_ref, ls.at[4]),
    ]
    for c in loads:
        c.start()
    barrier = pltpu.get_barrier_semaphore()

    for o in range(1, PA):
        pl.semaphore_signal(
            barrier, inc=1, device_id=(b, lax.rem(a + o, PA)), device_id_type=MESH
        )
    for o in range(1, PB):
        pl.semaphore_signal(
            barrier, inc=1, device_id=(lax.rem(b + o, PB), a), device_id_type=MESH
        )

    def group(k):
        return 2 * lax.rem(level + half - k // 2, half) + lax.rem(parity + k % 2, 2)

    def source(k):
        return 2 * lax.rem(level + k // 2, half) + lax.rem(parity + k % 2, 2)

    loads[0].wait()
    for q in range(queries):
        qh[q * token_local:(q + 1) * token_local] = qraw[q].astype(F32)
    loads[1].wait()
    qrows = qh[...].astype(BF)
    qe[a] = dot(qrows, proj[...], ((1,), (0,))).astype(BF)
    loads[2].wait()
    pe[b] = dot(ph[...], proj[...], ((1,), (0,))).astype(BF)
    pl.semaphore_wait(barrier, PB + PA - 2)

    query_in = []
    for o in range(1, PA):
        c = remote(qe.at[a], qe.at[a], qs.at[o - 1], qr.at[o - 1], b, lax.rem(a + o, PA))
        c.start()
        query_in.append(c)
    page_in = {}
    for k in range(PB - 1, 0, -1):
        c = remote(pe.at[b], pe.at[b], ps.at[k - 1], pr.at[k - 1], group(k), a)
        c.start()
        page_in[k] = c

    step = min(256, hidden)
    for s in range(0, hidden, step):
        pht[s:s + step] = ph[:, s:s + step].T

    for c in query_in:
        c.wait_recv()
    tok = qe[...].reshape(tokens, E)
    row = lax.broadcasted_iota(jnp.int32, (queries, tokens), 0) * token_local
    col = lax.broadcasted_iota(jnp.int32, (queries, tokens), 1)
    mask = jnp.zeros((queries, tokens), F32)
    for k in range(PA):
        low = row + k * rows
        mask = jnp.where((col >= low) & (col < low + token_local), 1.0, mask)
    maxes, sums = [], []
    for k in range(PB):
        if k:
            page_in[k].wait_recv()
        block = sharpness * dot(pe[source(k)], tok, ((1,), (1,)))
        top = jnp.max(block, axis=0, keepdims=True)
        e = jnp.exp(block - top)
        ebuf[k] = e
        maxes.append(top)
        sums.append(jnp.sum(e, axis=0, keepdims=True))
    top = functools.reduce(jnp.maximum, maxes)
    shrink = [jnp.exp(m - top) for m in maxes]
    total = functools.reduce(jnp.add, [s * f for s, f in zip(sums, shrink)])
    log_norm = top + jnp.log(total)
    score = jnp.sum(mask * log_norm, axis=1, keepdims=True)
    sc[a] = jnp.broadcast_to(score, sc.shape[1:])
    score_in = []
    for o in range(1, PA):
        c = remote(sc.at[a], sc.at[a], ss.at[o - 1], sr.at[o - 1], b, lax.rem(a + o, PA))
        c.start()
        score_in.append(c)

    unit = None
    for k in range(PB):
        soft = (ebuf[k] * (shrink[k] / total)).astype(BF)
        pbuf[k] = soft
        part = dot(soft, pe[source(k)], ((0,), (0,)))
        unit = part if unit is None else unit + part
    for k in range(PA):
        tsend[k] = unit[k * rows:(k + 1) * rows].astype(BF)
    token_in = []
    for o in range(1, PA):
        to = lax.rem(a + o, PA)
        c = remote(tsend.at[to], trecv.at[a], ts.at[o - 1], tr.at[o - 1], b, to)
        c.start()
        token_in.append(c)
    trecv[a] = tsend[a]

    loads[3].wait()
    loads[4].wait()
    pos = clicks_ref[:, 0, :]
    neg = clicks_ref[:, 1, :]
    pairs = pos.shape[1]
    weight = jnp.sqrt(bins_ref[...].astype(F32) + 1.0)
    for c in score_in:
        c.wait_recv()
    at_pos = jnp.zeros(pos.shape, F32)
    at_neg = jnp.zeros(pos.shape, F32)
    for p in range(PA):
        at_pos = at_pos + jnp.where(pos == p, sc[p][:, :pairs], 0.0)
        at_neg = at_neg + jnp.where(neg == p, sc[p][:, :pairs], 0.0)
    coeff = -weight * jax.nn.sigmoid(at_neg - at_pos)
    row = lax.broadcasted_iota(jnp.int32, (rows, queries), 0)
    col = lax.broadcasted_iota(jnp.int32, (rows, queries), 1) * token_local
    own = jnp.where((row >= col) & (row < col + token_local), 1.0, 0.0)

    def spread(page):
        hits = (pos == page).astype(F32) - (neg == page).astype(F32)
        grad = jnp.sum(coeff * hits, axis=1, keepdims=True)
        return sum(own[:, q:q + 1] * grad[q:q + 1] for q in range(queries))

    scaled = (qe[...].astype(F32) * spread(a)[None]).astype(BF).reshape(tokens, E)
    patch_in = []
    for k in range(PB - 1, -1, -1):
        patch_part = dot(pbuf[k], scaled, ((1,), (0,)))
        if k:
            gsend[k - 1] = patch_part.astype(BF)
            c = remote(
                gsend.at[k - 1], grecv.at[k - 1], gs.at[k - 1], gr.at[k - 1],
                source(k), a,
            )
            c.start()
            patch_in.append((k, c))
        else:
            patch_acc = patch_part

    for c in token_in:
        c.wait_recv()
    token_own = None
    for p in range(PA):
        part = trecv[p].astype(F32) * spread(p)
        token_own = part if token_own is None else token_own + part
    token_low = (sharpness * token_own).astype(BF)
    wq[...] = dot(qrows, token_low, ((0,), (0,)))
    qgrad = dot(token_low, proj[...], ((1,), (1,)))
    for q in range(queries):
        qg_ref[q] = qgrad[q * token_local:(q + 1) * token_local].astype(BF)

    for k, c in reversed(patch_in):
        c.wait_recv()
        patch_acc = patch_acc + grecv[k - 1].astype(F32)
    patch_low = (sharpness * patch_acc).astype(BF)

    partner = b + 1 - 2 * parity
    span = w1send.shape[1]
    chunk = w_ref.shape[0]
    def weight_block(index):
        base = pl.multiple_of(index * span, 8)
        return wq[pl.ds(base, span)] + dot(pht[pl.ds(base, span)], patch_low, ((1,), (0,)))

    pair_in = {}
    for m in range(half - 1, -1, -1):
        w1send[m] = weight_block(2 * lax.rem(level + m, half) + 1 - parity).astype(BF)
        c = remote(w1send.at[m], w1recv.at[m], us.at[m], ur.at[m], partner, a)
        c.start()
        pair_in[m] = c
    last_in = []
    weight_own = None
    for m in range(half - 1, -1, -1):
        to_level = lax.rem(level + m, half)
        mine = weight_block(2 * to_level + parity)
        pair_in[m].wait_recv()
        both = (mine + w1recv[m].astype(F32)).astype(BF)
        for k in range(PA):
            w2send[m * PA + k] = both[k * chunk:(k + 1) * chunk]
        for o in range(PA - 1, -1, -1):
            slot = m * PA + o
            if slot:
                to = lax.rem(a + o, PA)
                c = remote(
                    w2send.at[m * PA + to], w2recv.at[slot - 1], vs.at[slot - 1],
                    vr.at[slot - 1], 2 * to_level + parity, to,
                )
                c.start()
                last_in.append((slot, c))
    pg_ref[...] = dot(patch_low, proj[...], ((1,), (1,))).astype(BF)
    weight_sum = w2send[a].astype(F32)
    for slot, c in last_in:
        c.wait_recv()
        weight_sum = weight_sum + w2recv[slot - 1].astype(F32)
    w_ref[...] = weight_sum
    last_in = [c for _, c in last_in]
    pair_in = list(pair_in.values())
    for c in list(page_in.values()) + query_in + score_in + [c for _, c in patch_in] + token_in + pair_in + last_in:
        c.wait_send()


def writer(qg, pg, w, qg_out, pg_out, w_out, sems):
    copies = [
        pltpu.make_async_copy(pg, pg_out, sems.at[0]),
        pltpu.make_async_copy(qg, qg_out, sems.at[1]),
        pltpu.make_async_copy(w, w_out, sems.at[2]),
    ]
    for c in copies:
        c.start()
    for c in copies:
        c.wait()


def shards(PB, PA, query_hidden, page_hidden, projection, clicks, bins):
    queries, token_local, hidden = query_hidden.shape
    page_count, patches, _ = page_hidden.shape
    assert page_count == 1 and PB % 2 == 0
    E = projection.shape[1]
    rows = queries * token_local
    tokens = rows * PA
    chunk = hidden // (PB * PA)
    half = PB // 2
    count = half * PA
    ph = page_hidden.reshape(patches, hidden)
    vmem = pl.BlockSpec(memory_space=pltpu.VMEM)
    hbm = pl.BlockSpec(memory_space=pltpu.HBM)
    dma = lambda n: pltpu.SemaphoreType.DMA((n,))
    outs = (
        jax.ShapeDtypeStruct(query_hidden.shape, BF),
        jax.ShapeDtypeStruct((patches, hidden), BF),
        jax.ShapeDtypeStruct((chunk, E), F32),
    )
    results = pl.pallas_call(
        functools.partial(kernel, PB, PA),
        out_shape=tuple(pltpu.VMEM(o.shape, o.dtype) for o in outs),
        in_specs=[hbm] * 5,
        out_specs=(vmem,) * 3,
        scratch_shapes=[
            pltpu.VMEM((queries, 2, clicks.shape[1]), jnp.int32),
            pltpu.VMEM(bins.shape, jnp.int32),
            pltpu.VMEM(query_hidden.shape, BF),
            pltpu.VMEM((rows, hidden), F32),
            pltpu.VMEM((patches, hidden), BF),
            pltpu.VMEM((hidden, patches), BF),
            pltpu.VMEM((hidden, E), BF),
            pltpu.VMEM((PA, rows, E), BF),
            pltpu.VMEM((PB, patches, E), BF),
            pltpu.VMEM((PB, patches, tokens), F32),
            pltpu.VMEM((PB, patches, tokens), BF),
            pltpu.VMEM((PA, queries, 128), F32),
            pltpu.VMEM((PB - 1, patches, E), BF),
            pltpu.VMEM((PB - 1, patches, E), BF),
            pltpu.VMEM((PA, rows, E), BF),
            pltpu.VMEM((PA, rows, E), BF),
            pltpu.VMEM((hidden, E), F32),
            pltpu.VMEM((half, PA * chunk, E), BF),
            pltpu.VMEM((half, PA * chunk, E), BF),
            pltpu.VMEM((count, chunk, E), BF),
            pltpu.VMEM((count - 1, chunk, E), BF),
            dma(5), dma(PA - 1), dma(PA - 1), dma(PB - 1), dma(PB - 1), dma(PA - 1), dma(PA - 1),
            dma(PB - 1), dma(PB - 1), dma(PA - 1), dma(PA - 1), dma(half), dma(half),
            dma(count - 1), dma(count - 1),
        ],
        compiler_params=pltpu.CompilerParams(
            collective_id=0, has_side_effects=True, vmem_limit_bytes=65536000
        ),
        name="fused",
    )(query_hidden, ph, projection, jnp.transpose(clicks, (0, 2, 1)), bins)
    query_grad, page_grad, weight_grad = pl.pallas_call(
        writer,
        out_shape=outs,
        in_specs=[vmem] * 3,
        out_specs=(hbm,) * 3,
        scratch_shapes=[dma(3)],
        compiler_params=pltpu.CompilerParams(vmem_limit_bytes=4 * 1024 * 1024),
        name="writer",
    )(*results)
    return query_grad, page_grad.reshape(page_hidden.shape), weight_grad


def solution(mesh):
    return jax.shard_map(
        functools.partial(shards, mesh.shape["pb"], mesh.shape["pa"]),
        mesh=mesh,
        in_specs=(
            P("pb", "pa", None),
            P("pa", "pb", None),
            P(),
            P("pb", None, None),
            P("pb", None),
        ),
        out_specs=(P("pb", "pa", None), P("pa", "pb", None), P(("pb", "pa"), None)),
        check_vma=False,
    )
```

profile of v0, /device:TPU:0, one launch (start us, length us, event | category | flops | bytes accessed | tf_op | source)
XLA Modules:
  0.0 31.9 jit_solution(6915643921635424744)
XLA Ops:
  0.6 30.2 %fused.1 = (bf16[8,4,2048]{2,1,0:T(4,128)(2,1)S(1)}, bf16[256,2048]{1,0:T(8,128)(2,1)S(1)}, f32[64,128]{1,0:T(8,128)S(1)}) custom-call(bf16[8,4,2048]{2,1,0:T(4,128)(2,1)} %qh_hbm.1, bf16[256,2048]{1,0:T(8,128)(2,1)} %bitcast.3, bf16[2048,128]{1,0:T(8,128)(2,1)} %proj_hbm.1, s32[8,2,8]{2,1,0:T(2,128)} %bitcast.4, s32[8,8]{1,0:T(8,128)} %bins_hbm.1), custom_call_target="tpu_custom_call" | custom-call | tf_op jit(solution)/shard_map/fused/pallas_call | solution.py:271
  30.9 1.0 %writer.1 = (bf16[8,4,2048]{2,1,0:T(4,128)(2,1)}, bf16[256,2048]{1,0:T(8,128)(2,1)}, f32[64,128]{1,0:T(8,128)}) custom-call(bf16[8,4,2048]{2,1,0:T(4,128)(2,1)S(1)} %get-tuple-element.9.qg, bf16[256,2048]{1,0:T(8,128)(2,1)S(1)} %get-tuple-element.10.pg, f32[64,128]{1,0:T(8,128)S(1)} %get-tuple-element.11.w), custom_call_target="tpu_custom_call" | custom-call | tf_op jit(solution)/shard_map/writer/pallas_call | solution.py:307
where the time goes:
time: 32 us; the launch traced here: 31.9 us
  Pallas kernels  31.2 us (98%)
  between operations  0.64 us (2%)
    pallas_call x1, Pallas kernels, shards(): pl.pallas_call(functools.partial(kernel, PB, PA), out_shape=tuple((pltpu....  30.2 us
    pallas_call x1, Pallas kernels, shards(): pl.pallas_call(writer, out_shape=outs, in_specs=[vmem] * 3, out_specs=(hb...  1.03 us

commit v1 on v0

v1 whole, which is shorter than its diff:
```python
import functools
import math

import jax
import jax.numpy as jnp
from jax import lax
from jax.experimental import pallas as pl
from jax.experimental.pallas import tpu as pltpu
from jax.sharding import PartitionSpec as P

sharpness = 0.25
MESH = pl.DeviceIdType.MESH
BF = jnp.bfloat16
F32 = jnp.float32
FOLDED = sharpness * math.log2(math.e)
LOADS = 5
KINDS = ("query", "click", "bin", "page", "hidden", "raw", "norm", "token", "patch", "low", "weight")


def dot(x, y, dims):
    return lax.dot_general(x, y, (dims, ((), ())), preferred_element_type=F32)


def kernel(
    PB, PA, qh_hbm, ph_hbm, proj_hbm, clicks_hbm, bins_hbm,
    qg_ref, pg_ref, w_ref,
    clicks_ref, bins_ref, qraw, qh, qb, qx, ph, hx, pht, proj, qe, qt, pe, lbuf, ebuf, norm,
    tsend, trecv, gsend, grecv, low, wq, wsend, wrecv, sems,
):
    b = lax.axis_index("pb")
    a = lax.axis_index("pa")
    queries, token_local, hidden = qh_hbm.shape
    rows = queries * token_local
    patches = ph_hbm.shape[0]
    E = proj.shape[1]
    half = PB // 2
    slots = half * PA
    tokens = slots * rows
    total_queries = half * queries
    parity = lax.rem(b, 2)
    level = b // 2
    me = level * PA + a
    partner = (b + 1 - 2 * parity, a)
    chunk = w_ref.shape[0]
    span = PA * chunk
    width = 2 if PA < 32 else 4
    deep = PA // width
    z = a // width
    x = lax.rem(a, width)
    upper = z >= deep // 2

    def sem(kind, receive):
        return sems.at[LOADS + 2 * KINDS.index(kind) + receive]

    def remote(kind, src, dst, to):
        c = pltpu.make_async_remote_copy(
            src_ref=src, dst_ref=dst, send_sem=sem(kind, 0), recv_sem=sem(kind, 1),
            device_id=to, device_id_type=MESH,
        )
        c.start()

    def drain(kind, ref, receive):
        pltpu.make_async_copy(ref, ref, sem(kind, receive)).wait()

    def others(offsets):
        for i in range(deep):
            far = jnp.where(upper, i, deep - 1 - i)
            for k in offsets:
                to_level = lax.rem(level + k, half)
                for j in list(range(1, width)) + [0]:
                    to_z = far
                    if k == 0 and j == 0:
                        if i == deep - 1:
                            continue
                        up = i + jnp.where(i >= z, 1, 0)
                        down = deep - 1 - i - jnp.where(deep - 1 - i <= z, 1, 0)
                        to_z = jnp.where(upper, up, down)
                    yield to_level, to_z * width + lax.rem(x + j, width)

    every = list(range(1, half)) + [0]

    def device(to_level, to_a):
        return 2 * to_level + parity, to_a

    loads = [
        pltpu.make_async_copy(qh_hbm, qraw, sems.at[0]),
        pltpu.make_async_copy(proj_hbm, proj, sems.at[1]),
        pltpu.make_async_copy(ph_hbm, ph, sems.at[2]),
        pltpu.make_async_copy(clicks_hbm, clicks_ref.at[level], sems.at[3]),
        pltpu.make_async_copy(bins_hbm, bins_ref.at[level], sems.at[4]),
    ]
    for c in loads:
        c.start()
    barrier = pltpu.get_barrier_semaphore()
    for to in others(every):
        pl.semaphore_signal(barrier, inc=1, device_id=device(*to), device_id_type=MESH)
    pl.semaphore_signal(barrier, inc=1, device_id=partner, device_id_type=MESH)

    loads[0].wait()
    for q in range(queries):
        qh[q * token_local:(q + 1) * token_local] = qraw[q].astype(F32)
    qb[...] = qh[...].astype(BF)
    loads[1].wait()
    qe[me] = dot(qb[...], proj[...], ((1,), (0,))).astype(BF)
    pl.semaphore_wait(barrier, slots)
    for to in others(every):
        remote("query", qe.at[me], qe.at[me], device(*to))
    for k in range(1, half):
        to = device(lax.rem(level + k, half), a)
        remote("click", clicks_hbm, clicks_ref.at[level], to)
        remote("bin", bins_hbm, bins_ref.at[level], to)

    loads[2].wait()
    pe[0] = dot(ph[...], proj[...], ((1,), (0,))).astype(BF)
    remote("page", pe.at[0], pe.at[1], partner)

    def columns(l, core):
        return pl.ds(pl.multiple_of((2 * l + core) * span, 128), span)

    for l in range(half):
        remote("hidden", ph.at[:, columns(l, 1 - parity)], hx.at[l], partner)
        remote("raw", qb.at[:, columns(l, 1 - parity)], qx.at[l], partner)

    query_of = lax.broadcasted_iota(jnp.int32, (total_queries, tokens), 0)
    token_of = lax.broadcasted_iota(jnp.int32, (total_queries, tokens), 1)

    def belongs(query_id, token_id):
        own_query = lax.rem(token_id, rows) // token_local + token_id // (PA * rows) * queries
        return jnp.where(query_id == own_query, 1.0, 0.0)

    mask = belongs(query_of, token_of)
    for l in range(half):
        pht[l, 0] = ph[:, columns(l, parity)].T
    drain("hidden", hx, 1)
    for l in range(half):
        pht[l, 1] = hx[l].T

    drain("page", pe.at[0], 1)
    drain("query", qe.at[pl.ds(0, slots - 1)], 1)
    tok = qe[...].reshape(tokens, E)
    top = None
    for k in range(2):
        block = dot(pe[k], tok, ((1,), (1,)))
        lbuf[k] = block
        high = jnp.max(block, axis=0, keepdims=True)
        top = high if top is None else jnp.maximum(top, high)
    total = None
    for k in range(2):
        e = jnp.exp2((lbuf[k] - top) * FOLDED)
        ebuf[k] = e.astype(BF)
        part = jnp.sum(e, axis=0, keepdims=True)
        total = part if total is None else total + part
    top = sharpness * top
    norm[me] = top + jnp.log(total)
    for to in others(every):
        remote("norm", norm.at[me], norm.at[me], device(*to))

    unit = dot(pe[0], ebuf[0], ((0,), (0,))) + dot(pe[1], ebuf[1], ((0,), (0,)))
    unit = (unit / total).T.astype(BF)
    for s in range(slots):
        tsend[s] = unit[s * rows:(s + 1) * rows]
    for to_level, to_a in others(every):
        remote("token", tsend.at[to_level * PA + to_a], trecv.at[me], device(to_level, to_a))
    trecv[me] = tsend[me]
    qt[...] = tok.astype(F32).T

    loads[3].wait()
    loads[4].wait()
    if half > 1:
        drain("click", clicks_ref.at[pl.ds(0, half - 1)], 1)
        drain("bin", bins_ref.at[pl.ds(0, half - 1)], 1)
    pairs = bins_ref.shape[2]
    pos = clicks_ref[:, :, 0, :].reshape(total_queries, pairs)
    neg = clicks_ref[:, :, 1, :].reshape(total_queries, pairs)
    weight = jnp.sqrt(bins_ref[...].reshape(total_queries, pairs).astype(F32) + 1.0)

    def merged(parts):
        high = functools.reduce(jnp.maximum, parts)
        return high + jnp.log(functools.reduce(jnp.add, [jnp.exp(v - high) for v in parts]))

    drain("norm", norm.at[pl.ds(0, slots - 1)], 1)
    at_pos = jnp.zeros(pos.shape, F32)
    at_neg = jnp.zeros(pos.shape, F32)
    for p in range(PA):
        log_norm = merged([norm[l * PA + p] for l in range(half)])
        score = jnp.sum(mask * log_norm, axis=1, keepdims=True)
        at_pos = at_pos + jnp.where(pos == p, score, 0.0)
        at_neg = at_neg + jnp.where(neg == p, score, 0.0)
    coeff = -weight * jax.nn.sigmoid(at_neg - at_pos)

    def score_grad(page):
        hits = (pos == page).astype(F32) - (neg == page).astype(F32)
        return jnp.sum(coeff * hits, axis=1, keepdims=True)

    log_norm = merged([norm[l * PA + a] for l in range(half)])
    factor = jnp.sum(mask * score_grad(a), axis=0, keepdims=True) * jnp.exp(top - log_norm)
    scaled = (qt[...] * factor).astype(BF)
    mine = []
    for k in range(2):
        part = dot(scaled, ebuf[k], ((1,), (1,)))
        gsend[k] = part.astype(BF)
        mine.append(part)
    remote("patch", gsend, grecv, partner)

    lanes = min(128, tokens)
    near = pl.ds(pl.multiple_of(me * rows // lanes * lanes, lanes), lanes)
    first = me * rows // lanes * lanes
    own_mask = belongs(
        lax.broadcasted_iota(jnp.int32, (total_queries, lanes), 0),
        first + lax.broadcasted_iota(jnp.int32, (total_queries, lanes), 1),
    )
    pick = jnp.where(
        lax.broadcasted_iota(jnp.int32, (rows, lanes), 0) + (me * rows - first)
        == lax.broadcasted_iota(jnp.int32, (rows, lanes), 1), 1.0, 0.0,
    )
    drain("token", trecv.at[pl.ds(0, slots - 1)], 1)
    token_own = None
    for p in range(PA):
        parts = [norm[l * PA + p, :, near] for l in range(half)]
        log_norm = merged(parts)
        grad = jnp.sum(own_mask * score_grad(p), axis=0, keepdims=True)
        for l in range(half):
            share = jnp.sum(pick * (grad * jnp.exp(parts[l] - log_norm)), axis=1, keepdims=True)
            part = trecv[l * PA + p].astype(F32) * share
            token_own = part if token_own is None else token_own + part
    token_low = (sharpness * token_own).astype(BF)
    low[0] = token_low
    remote("low", low.at[0], low.at[1], partner)

    drain("raw", qx, 1)
    drain("low", low.at[0], 1)
    for l in range(half):
        wq[l] = dot(qb[:, columns(l, parity)], token_low, ((0,), (0,))) + dot(qx[l], low[1], ((0,), (0,)))

    drain("patch", grecv, 1)
    patch_low = [(sharpness * (mine[k] + grecv[1 - k].astype(F32))).astype(BF) for k in range(2)]

    for k in every:
        to_level = lax.rem(level + k, half)
        block = wq[to_level]
        for i in range(2):
            block = block + dot(pht[to_level, i], patch_low[i], ((1,), (1,)))
        block = block.astype(BF)
        for s in range(PA):
            wsend[to_level * PA + s] = block[s * chunk:(s + 1) * chunk]
        for _, to_a in others([k]):
            remote("weight", wsend.at[to_level * PA + to_a], wrecv.at[me], device(to_level, to_a))
    wrecv[me] = wsend[me]

    qgrad = dot(token_low, proj[...], ((1,), (1,)))
    for q in range(queries):
        qg_ref[q] = qgrad[q * token_local:(q + 1) * token_local].astype(BF)
    pg_ref[...] = dot(patch_low[0].T, proj[...], ((1,), (1,))).astype(BF)

    drain("query", qe.at[pl.ds(0, slots - 1)], 0)
    if half > 1:
        drain("click", clicks_ref.at[pl.ds(0, half - 1)], 0)
        drain("bin", bins_ref.at[pl.ds(0, half - 1)], 0)
    drain("page", pe.at[0], 0)
    drain("hidden", hx, 0)
    drain("raw", qx, 0)
    drain("norm", norm.at[pl.ds(0, slots - 1)], 0)
    drain("token", tsend.at[pl.ds(0, slots - 1)], 0)
    drain("patch", gsend, 0)
    drain("low", low.at[0], 0)
    drain("weight", wsend.at[pl.ds(0, slots - 1)], 0)
    drain("weight", wrecv.at[pl.ds(0, slots - 1)], 1)
    weight_sum = wrecv[0].astype(F32)
    for s in range(1, slots):
        weight_sum = weight_sum + wrecv[s].astype(F32)
    w_ref[...] = weight_sum


def writer(qg, pg, w, qg_out, pg_out, w_out, sems):
    copies = [
        pltpu.make_async_copy(pg, pg_out, sems.at[0]),
        pltpu.make_async_copy(qg, qg_out, sems.at[1]),
        pltpu.make_async_copy(w, w_out, sems.at[2]),
    ]
    for c in copies:
        c.start()
    for c in copies:
        c.wait()


def shards(PB, PA, query_hidden, page_hidden, projection, clicks, bins):
    queries, token_local, hidden = query_hidden.shape
    page_count, patches, _ = page_hidden.shape
    assert page_count == 1 and PB % 2 == 0
    E = projection.shape[1]
    rows = queries * token_local
    half = PB // 2
    slots = half * PA
    tokens = rows * slots
    chunk = hidden // (PB * PA)
    span = PA * chunk
    pairs = clicks.shape[1]
    ph = page_hidden.reshape(patches, hidden)
    vmem = pl.BlockSpec(memory_space=pltpu.VMEM)
    hbm = pl.BlockSpec(memory_space=pltpu.HBM)
    dma = lambda n: pltpu.SemaphoreType.DMA((n,))
    outs = (
        jax.ShapeDtypeStruct(query_hidden.shape, BF),
        jax.ShapeDtypeStruct((patches, hidden), BF),
        jax.ShapeDtypeStruct((chunk, E), F32),
    )
    results = pl.pallas_call(
        functools.partial(kernel, PB, PA),
        out_shape=tuple(pltpu.VMEM(o.shape, o.dtype) for o in outs),
        in_specs=[hbm] * 5,
        out_specs=(vmem,) * 3,
        scratch_shapes=[
            pltpu.VMEM((half, queries, 2, pairs), jnp.int32),
            pltpu.VMEM((half, queries, pairs), jnp.int32),
            pltpu.VMEM(query_hidden.shape, BF),
            pltpu.VMEM((rows, hidden), F32),
            pltpu.VMEM((rows, hidden), BF),
            pltpu.VMEM((half, rows, span), BF),
            pltpu.VMEM((patches, hidden), BF),
            pltpu.VMEM((half, patches, span), BF),
            pltpu.VMEM((half, 2, span, patches), BF),
            pltpu.VMEM((hidden, E), BF),
            pltpu.VMEM((slots, rows, E), BF),
            pltpu.VMEM((E, tokens), F32),
            pltpu.VMEM((2, patches, E), BF),
            pltpu.VMEM((2, patches, tokens), F32),
            pltpu.VMEM((2, patches, tokens), BF),
            pltpu.VMEM((slots, 1, tokens), F32),
            pltpu.VMEM((slots, rows, E), BF),
            pltpu.VMEM((slots, rows, E), BF),
            pltpu.VMEM((2, E, patches), BF),
            pltpu.VMEM((2, E, patches), BF),
            pltpu.VMEM((2, rows, E), BF),
            pltpu.VMEM((half, span, E), F32),
            pltpu.VMEM((slots, chunk, E), BF),
            pltpu.VMEM((slots, chunk, E), BF),
            dma(LOADS + 2 * len(KINDS)),
        ],
        compiler_params=pltpu.CompilerParams(
            collective_id=0, has_side_effects=True, vmem_limit_bytes=65536000
        ),
        name="fused",
    )(query_hidden, ph, projection, jnp.transpose(clicks, (0, 2, 1)), bins)
    query_grad, page_grad, weight_grad = pl.pallas_call(
        writer,
        out_shape=outs,
        in_specs=[vmem] * 3,
        out_specs=(hbm,) * 3,
        scratch_shapes=[dma(3)],
        compiler_params=pltpu.CompilerParams(vmem_limit_bytes=4 * 1024 * 1024),
        name="writer",
    )(*results)
    return query_grad, page_grad.reshape(page_hidden.shape), weight_grad


def solution(mesh):
    return jax.shard_map(
        functools.partial(shards, mesh.shape["pb"], mesh.shape["pa"]),
        mesh=mesh,
        in_specs=(
            P("pb", "pa", None),
            P("pa", "pb", None),
            P(),
            P("pb", None, None),
            P("pb", None),
        ),
        out_specs=(P("pb", "pa", None), P("pa", "pb", None), P(("pb", "pa"), None)),
        check_vma=False,
    )
```

time: 32 us -> 27.8 us (0.87)
  Pallas kernels: 31.2 us -> 27 us
    pallas_call x1, Pallas kernels: 30.2 us -> 26 us  [shards(): pl.pallas_call(functools.partial(kernel, PB, PA), out_shape=tuple((pltpu....]
where the time goes in v1:
time: 27.8 us; the launch traced here: 27.6 us
  Pallas kernels  27 us (97%)
  between operations  0.64 us (2%)
    pallas_call x1, Pallas kernels, shards(): pl.pallas_call(functools.partial(kernel, PB, PA), out_shape=tuple((pltpu....  26 us
    pallas_call x1, Pallas kernels, shards(): pl.pallas_call(writer, out_shape=outs, in_specs=[vmem] * 3, out_specs=(hb...  1.03 us

profile of v1, /device:TPU:0, one launch (start us, length us, event | category | flops | bytes accessed | tf_op | source)
XLA Modules:
  0.0 27.6 jit_solution(8731934877822280280)
XLA Ops:
  0.6 26.0 %fused.1 = (bf16[8,4,2048]{2,1,0:T(4,128)(2,1)S(1)}, bf16[256,2048]{1,0:T(8,128)(2,1)S(1)}, f32[64,128]{1,0:T(8,128)S(1)}) custom-call(bf16[8,4,2048]{2,1,0:T(4,128)(2,1)} %qh_hbm.1, bf16[256,2048]{1,0:T(8,128)(2,1)} %bitcast.3, bf16[2048,128]{1,0:T(8,128)(2,1)} %proj_hbm.1, s32[8,2,8]{2,1,0:T(2,128)} %bitcast.4, s32[8,8]{1,0:T(8,128)} %bins_hbm.1), custom_call_target="tpu_custom_call" | custom-call | tf_op jit(solution)/shard_map/fused/pallas_call | solution.py:307
  26.6 1.0 %writer.1 = (bf16[8,4,2048]{2,1,0:T(4,128)(2,1)}, bf16[256,2048]{1,0:T(8,128)(2,1)}, f32[64,128]{1,0:T(8,128)}) custom-call(bf16[8,4,2048]{2,1,0:T(4,128)(2,1)S(1)} %get-tuple-element.9.qg, bf16[256,2048]{1,0:T(8,128)(2,1)S(1)} %get-tuple-element.10.pg, f32[64,128]{1,0:T(8,128)S(1)} %get-tuple-element.11.w), custom_call_target="tpu_custom_call" | custom-call | tf_op jit(solution)/shard_map/writer/pallas_call | solution.py:344

commit v2 on v1

--- a/solution.py
+++ b/solution.py
@@ -14,7 +14,7 @@
 F32 = jnp.float32
 FOLDED = sharpness * math.log2(math.e)
 LOADS = 5
-KINDS = ("query", "click", "bin", "page", "hidden", "raw", "norm", "token", "patch", "low", "weight")
+KINDS = ("query", "query_far", "click", "bin", "page", "hidden", "raw", "norm", "token", "patch", "low", "weight")
 
 
 def dot(x, y, dims):
@@ -24,7 +24,7 @@
 def kernel(
     PB, PA, qh_hbm, ph_hbm, proj_hbm, clicks_hbm, bins_hbm,
     qg_ref, pg_ref, w_ref,
-    clicks_ref, bins_ref, qraw, qh, qb, qx, ph, hx, pht, proj, qe, qt, pe, lbuf, ebuf, norm,
+    clicks_ref, bins_ref, qraw, qh, qb, qx, ph, hx, pht, proj, qe, qt, pe, lbuf, ebuf, ebt, tops, totals, norm,
     tsend, trecv, gsend, grecv, low, wq, wsend, wrecv, sems,
 ):
     b = lax.axis_index("pb")
@@ -52,9 +52,9 @@
     def sem(kind, receive):
         return sems.at[LOADS + 2 * KINDS.index(kind) + receive]
 
-    def remote(kind, src, dst, to):
+    def remote(kind, src, dst, to, received=None):
         c = pltpu.make_async_remote_copy(
-            src_ref=src, dst_ref=dst, send_sem=sem(kind, 0), recv_sem=sem(kind, 1),
+            src_ref=src, dst_ref=dst, send_sem=sem(kind, 0), recv_sem=received or sem(kind, 1),
             device_id=to, device_id_type=MESH,
         )
         c.start()
@@ -82,6 +82,11 @@
     def device(to_level, to_a):
         return 2 * to_level + parity, to_a
 
+    barrier = pltpu.get_barrier_semaphore()
+    for to in others(every):
+        pl.semaphore_signal(barrier, inc=1, device_id=device(*to), device_id_type=MESH)
+    pl.semaphore_signal(barrier, inc=1, device_id=partner, device_id_type=MESH)
+
     loads = [
         pltpu.make_async_copy(qh_hbm, qraw, sems.at[0]),
         pltpu.make_async_copy(proj_hbm, proj, sems.at[1]),
@@ -91,11 +96,6 @@
     ]
     for c in loads:
         c.start()
-    barrier = pltpu.get_barrier_semaphore()
-    for to in others(every):
-        pl.semaphore_signal(barrier, inc=1, device_id=device(*to), device_id_type=MESH)
-    pl.semaphore_signal(barrier, inc=1, device_id=partner, device_id_type=MESH)
-
     loads[0].wait()
     for q in range(queries):
         qh[q * token_local:(q + 1) * token_local] = qraw[q].astype(F32)
@@ -103,8 +103,11 @@
     loads[1].wait()
     qe[me] = dot(qb[...], proj[...], ((1,), (0,))).astype(BF)
     pl.semaphore_wait(barrier, slots)
+    group = PA // 2
+    side = a // group
     for to in others(every):
-        remote("query", qe.at[me], qe.at[me], device(*to))
+        other_side = jnp.where(to[1] // group == side, 0, 1)
+        remote("query", qe.at[me], qe.at[me], device(*to), sems.at[LOADS + 1 + 2 * other_side])
     for k in range(1, half):
         to = device(lax.rem(level + k, half), a)
         remote("click", clicks_hbm, clicks_ref.at[level], to)
@@ -136,33 +139,42 @@
         pht[l, 1] = hx[l].T
 
     drain("page", pe.at[0], 1)
-    drain("query", qe.at[pl.ds(0, slots - 1)], 1)
-    tok = qe[...].reshape(tokens, E)
-    top = None
-    for k in range(2):
-        block = dot(pe[k], tok, ((1,), (1,)))
-        lbuf[k] = block
-        high = jnp.max(block, axis=0, keepdims=True)
-        top = high if top is None else jnp.maximum(top, high)
-    total = None
-    for k in range(2):
-        e = jnp.exp2((lbuf[k] - top) * FOLDED)
-        ebuf[k] = e.astype(BF)
-        part = jnp.sum(e, axis=0, keepdims=True)
-        total = part if total is None else total + part
-    top = sharpness * top
-    norm[me] = top + jnp.log(total)
+    part_tokens = group * rows
+    for near in (True, False):
+        drain("query" if near else "query_far", qe.at[pl.ds(0, half * group - near)], 1)
+        for l in range(half):
+            start = l * PA + group * (side if near else 1 - side)
+            lanes = pl.ds(pl.multiple_of(start * rows, 128), part_tokens)
+            tok = qe[pl.ds(start, group)].reshape(part_tokens, E)
+            top = None
+            for k in range(2):
+                block = dot(pe[k], tok, ((1,), (1,)))
+                lbuf[k] = block
+                high = jnp.max(block, axis=0, keepdims=True)
+                top = high if top is None else jnp.maximum(top, high)
+            total = None
+            for k in range(2):
+                e = jnp.exp2((lbuf[k] - top) * FOLDED)
+                ebuf[k, :, lanes] = e.astype(BF)
+                part = jnp.sum(e, axis=0, keepdims=True)
+                total = part if total is None else total + part
+            top = sharpness * top
+            tops[:, lanes] = top
+            totals[:, lanes] = total
+            norm[me, :, lanes] = top + jnp.log(total)
     for to in others(every):
         remote("norm", norm.at[me], norm.at[me], device(*to))
 
     unit = dot(pe[0], ebuf[0], ((0,), (0,))) + dot(pe[1], ebuf[1], ((0,), (0,)))
-    unit = (unit / total).T.astype(BF)
+    unit = (unit / totals[...]).T.astype(BF)
     for s in range(slots):
         tsend[s] = unit[s * rows:(s + 1) * rows]
     for to_level, to_a in others(every):
         remote("token", tsend.at[to_level * PA + to_a], trecv.at[me], device(to_level, to_a))
     trecv[me] = tsend[me]
-    qt[...] = tok.astype(F32).T
+    qt[...] = qe[...].reshape(tokens, E).astype(F32).T
+    for k in range(2):
+        ebt[k] = ebuf[k].T
 
     loads[3].wait()
     loads[4].wait()
@@ -181,9 +193,10 @@
     drain("norm", norm.at[pl.ds(0, slots - 1)], 1)
     at_pos = jnp.zeros(pos.shape, F32)
     at_neg = jnp.zeros(pos.shape, F32)
+    rows_in = norm[...].reshape(slots, tokens)
+    log_norms = merged([rows_in[l * PA:(l + 1) * PA] for l in range(half)])
     for p in range(PA):
-        log_norm = merged([norm[l * PA + p] for l in range(half)])
-        score = jnp.sum(mask * log_norm, axis=1, keepdims=True)
+        score = jnp.sum(mask * log_norms[p:p + 1], axis=1, keepdims=True)
         at_pos = at_pos + jnp.where(pos == p, score, 0.0)
         at_neg = at_neg + jnp.where(neg == p, score, 0.0)
     coeff = -weight * jax.nn.sigmoid(at_neg - at_pos)
@@ -193,18 +206,18 @@
         return jnp.sum(coeff * hits, axis=1, keepdims=True)
 
     log_norm = merged([norm[l * PA + a] for l in range(half)])
-    factor = jnp.sum(mask * score_grad(a), axis=0, keepdims=True) * jnp.exp(top - log_norm)
+    factor = jnp.sum(mask * score_grad(a), axis=0, keepdims=True) * jnp.exp(tops[...] - log_norm)
     scaled = (qt[...] * factor).astype(BF)
     mine = []
     for k in range(2):
-        part = dot(scaled, ebuf[k], ((1,), (1,)))
+        part = dot(scaled, ebt[k], ((1,), (0,)))
         gsend[k] = part.astype(BF)
+        remote("patch", gsend.at[k], grecv.at[k], partner)
         mine.append(part)
-    remote("patch", gsend, grecv, partner)
 
     lanes = min(128, tokens)
-    near = pl.ds(pl.multiple_of(me * rows // lanes * lanes, lanes), lanes)
     first = me * rows // lanes * lanes
+    near = pl.ds(pl.multiple_of(first, lanes), lanes)
     own_mask = belongs(
         lax.broadcasted_iota(jnp.int32, (total_queries, lanes), 0),
         first + lax.broadcasted_iota(jnp.int32, (total_queries, lanes), 1),
@@ -213,16 +226,23 @@
         lax.broadcasted_iota(jnp.int32, (rows, lanes), 0) + (me * rows - first)
         == lax.broadcasted_iota(jnp.int32, (rows, lanes), 1), 1.0, 0.0,
     )
+    page_of = lax.broadcasted_iota(jnp.int32, (PA, lanes), 0)
+    grads = jnp.zeros((PA, lanes), F32)
+    for p in range(PA):
+        grads = jnp.where(page_of == p, jnp.sum(own_mask * score_grad(p), axis=0, keepdims=True), grads)
+    rows_in = norm[:, :, near].reshape(slots, lanes)
+    parts = [rows_in[l * PA:(l + 1) * PA] for l in range(half)]
+    log_norms = merged(parts)
+    shares = []
+    for l in range(half):
+        factors = grads * jnp.exp(parts[l] - log_norms)
+        for p in range(PA):
+            shares.append(jnp.sum(pick * factors[p:p + 1], axis=1, keepdims=True))
     drain("token", trecv.at[pl.ds(0, slots - 1)], 1)
     token_own = None
-    for p in range(PA):
-        parts = [norm[l * PA + p, :, near] for l in range(half)]
-        log_norm = merged(parts)
-        grad = jnp.sum(own_mask * score_grad(p), axis=0, keepdims=True)
-        for l in range(half):
-            share = jnp.sum(pick * (grad * jnp.exp(parts[l] - log_norm)), axis=1, keepdims=True)
-            part = trecv[l * PA + p].astype(F32) * share
-            token_own = part if token_own is None else token_own + part
+    for s in range(slots):
+        part = trecv[s].astype(F32) * shares[s]
+        token_own = part if token_own is None else token_own + part
     token_low = (sharpness * token_own).astype(BF)
     low[0] = token_low
     remote("low", low.at[0], low.at[1], partner)
@@ -233,24 +253,24 @@
         wq[l] = dot(qb[:, columns(l, parity)], token_low, ((0,), (0,))) + dot(qx[l], low[1], ((0,), (0,)))
 
     drain("patch", grecv, 1)
-    patch_low = [(sharpness * (mine[k] + grecv[1 - k].astype(F32))).astype(BF) for k in range(2)]
+    patch_low = [(sharpness * (mine[k] + grecv[1 - k].astype(F32))).astype(BF).T for k in range(2)]
 
     for k in every:
         to_level = lax.rem(level + k, half)
         block = wq[to_level]
         for i in range(2):
-            block = block + dot(pht[to_level, i], patch_low[i], ((1,), (1,)))
+            block = block + dot(pht[to_level, i], patch_low[i], ((1,), (0,)))
         block = block.astype(BF)
         for s in range(PA):
             wsend[to_level * PA + s] = block[s * chunk:(s + 1) * chunk]
-        for _, to_a in others([k]):
-            remote("weight", wsend.at[to_level * PA + to_a], wrecv.at[me], device(to_level, to_a))
+    for to_level, to_a in others(every):
+        remote("weight", wsend.at[to_level * PA + to_a], wrecv.at[me], device(to_level, to_a))
     wrecv[me] = wsend[me]
 
     qgrad = dot(token_low, proj[...], ((1,), (1,)))
     for q in range(queries):
         qg_ref[q] = qgrad[q * token_local:(q + 1) * token_local].astype(BF)
-    pg_ref[...] = dot(patch_low[0].T, proj[...], ((1,), (1,))).astype(BF)
+    pg_ref[...] = dot(patch_low[0], proj[...], ((1,), (1,))).astype(BF)
 
     drain("query", qe.at[pl.ds(0, slots - 1)], 0)
     if half > 1:
@@ -323,8 +343,11 @@
             pltpu.VMEM((slots, rows, E), BF),
             pltpu.VMEM((E, tokens), F32),
             pltpu.VMEM((2, patches, E), BF),
-            pltpu.VMEM((2, patches, tokens), F32),
+            pltpu.VMEM((2, patches, tokens // half // 2), F32),
             pltpu.VMEM((2, patches, tokens), BF),
+            pltpu.VMEM((2, tokens, patches), BF),
+            pltpu.VMEM((1, tokens), F32),
+            pltpu.VMEM((1, tokens), F32),
             pltpu.VMEM((slots, 1, tokens), F32),
             pltpu.VMEM((slots, rows, E), BF),
             pltpu.VMEM((slots, rows, E), BF),

time: 27.8 us -> 27.1 us (0.975)
  Pallas kernels: 27 us -> 26.2 us
    pallas_call x1, Pallas kernels: 26 us -> 25.2 us  [shards(): pl.pallas_call(functools.partial(kernel, PB, PA), out_shape=tuple((pltpu....]
where the time goes in v2:
time: 27.1 us; the launch traced here: 26.9 us
  Pallas kernels  26.2 us (97%)
  between operations  0.64 us (2%)
    pallas_call x1, Pallas kernels, shards(): pl.pallas_call(functools.partial(kernel, PB, PA), out_shape=tuple((pltpu....  25.2 us
    pallas_call x1, Pallas kernels, shards(): pl.pallas_call(writer, out_shape=outs, in_specs=[vmem] * 3, out_specs=(hb...  1.03 us

profile of v2, /device:TPU:0, one launch (start us, length us, event | category | flops | bytes accessed | tf_op | source)
XLA Modules:
  0.0 26.9 jit_solution(567041082512452595)
XLA Ops:
  0.6 25.2 %fused.1 = (bf16[8,4,2048]{2,1,0:T(4,128)(2,1)S(1)}, bf16[256,2048]{1,0:T(8,128)(2,1)S(1)}, f32[64,128]{1,0:T(8,128)S(1)}) custom-call(bf16[8,4,2048]{2,1,0:T(4,128)(2,1)} %qh_hbm.1, bf16[256,2048]{1,0:T(8,128)(2,1)} %bitcast.3, bf16[2048,128]{1,0:T(8,128)(2,1)} %proj_hbm.1, s32[8,2,8]{2,1,0:T(2,128)} %bitcast.4, s32[8,8]{1,0:T(8,128)} %bins_hbm.1), custom_call_target="tpu_custom_call" | custom-call | tf_op jit(solution)/shard_map/fused/pallas_call | solution.py:327
  25.9 1.0 %writer.1 = (bf16[8,4,2048]{2,1,0:T(4,128)(2,1)}, bf16[256,2048]{1,0:T(8,128)(2,1)}, f32[64,128]{1,0:T(8,128)}) custom-call(bf16[8,4,2048]{2,1,0:T(4,128)(2,1)S(1)} %get-tuple-element.9.qg, bf16[256,2048]{1,0:T(8,128)(2,1)S(1)} %get-tuple-element.10.pg, f32[64,128]{1,0:T(8,128)S(1)} %get-tuple-element.11.w), custom_call_target="tpu_custom_call" | custom-call | tf_op jit(solution)/shard_map/writer/pallas_call | solution.py:367

commit v3 on v1

v3 whole, which is shorter than its diff:
```python
import functools
import math

import jax
import jax.numpy as jnp
from jax import lax
from jax.experimental import pallas as pl
from jax.experimental.pallas import tpu as pltpu
from jax.sharding import PartitionSpec as P

sharpness = 0.25
MESH = pl.DeviceIdType.MESH
BF = jnp.bfloat16
F32 = jnp.float32
FOLDED = sharpness * math.log2(math.e)
RECEIVED = (
    "near", "far", "click", "bin", "page", "other", "hidden", "raw", "level", "norm", "token", "patch", "low", "weight",
)
LOADS = 5


def dot(x, y, dims):
    return lax.dot_general(x, y, (dims, ((), ())), preferred_element_type=F32)


def kernel(
    PB, PA, qh_hbm, ph_hbm, proj_hbm, clicks_hbm, bins_hbm,
    qg_ref, pg_ref, w_ref,
    clicks_ref, bins_ref, qraw, qh, qb, qx, ph, hx, pht, proj, qe, qt, pe, po, lbuf, ebuf, ebt, eo, tops, sums, norm,
    tsend, trecv, gsend, grecv, low, wq, wsend, wrecv, arrived,
):
    b = lax.axis_index("pb")
    a = lax.axis_index("pa")
    queries, token_local, hidden = qh_hbm.shape
    rows = queries * token_local
    patches = ph_hbm.shape[0]
    E = proj.shape[1]
    half = PB // 2
    slots = half * PA
    level_tokens = PA * rows
    tokens = half * level_tokens
    parity = lax.rem(b, 2)
    level = b // 2
    me = level * PA + a
    partner = (b + 1 - 2 * parity, a)
    chunk = w_ref.shape[0]
    span = PA * chunk
    width = 2 if PA < 32 else 4
    deep = PA // width
    z = a // width
    x = lax.rem(a, width)
    upper = z >= deep // 2
    group = PA // 2
    side = a // group

    def others(offsets):
        for i in range(deep):
            far = jnp.where(upper, i, deep - 1 - i)
            for k in offsets:
                to_level = lax.rem(level + k, half)
                for j in list(range(1, width)) + [0]:
                    to_z = far
                    if k == 0 and j == 0:
                        if i == deep - 1:
                            continue
                        up = i + jnp.where(i >= z, 1, 0)
                        down = deep - 1 - i - jnp.where(deep - 1 - i <= z, 1, 0)
                        to_z = jnp.where(upper, up, down)
                    yield to_level, to_z * width + lax.rem(x + j, width)

    every = list(range(1, half)) + [0]

    def device(to_level, to_a):
        return 2 * to_level + parity, to_a

    def across(k):
        to_level = lax.rem(level + k, half)
        return device(to_level, a), (2 * to_level + 1 - parity, a)

    barrier = pltpu.get_barrier_semaphore()
    for to in others([0]):
        pl.semaphore_signal(barrier, inc=1, device_id=device(*to), device_id_type=MESH)
    for k in range(1, half):
        for to in across(k):
            pl.semaphore_signal(barrier, inc=1, device_id=to, device_id_type=MESH)
    pl.semaphore_signal(barrier, inc=1, device_id=partner, device_id_type=MESH)

    def body(sent):
        def remote(kind, src, dst, to, received=None):
            pltpu.make_async_remote_copy(
                src_ref=src, dst_ref=dst, send_sem=sent.at[LOADS + RECEIVED.index(kind)],
                recv_sem=arrived.at[RECEIVED.index(kind)] if received is None else received,
                device_id=to, device_id_type=MESH,
            ).start()

        def receive(kind, ref):
            pltpu.make_async_copy(ref, ref, arrived.at[RECEIVED.index(kind)]).wait()

        def flush(kind, ref):
            pltpu.make_async_copy(ref, ref, sent.at[LOADS + RECEIVED.index(kind)]).wait()

        loads = [
            pltpu.make_async_copy(qh_hbm, qraw, sent.at[0]),
            pltpu.make_async_copy(proj_hbm, proj, sent.at[1]),
            pltpu.make_async_copy(ph_hbm, ph, sent.at[2]),
            pltpu.make_async_copy(clicks_hbm, clicks_ref.at[level], sent.at[3]),
            pltpu.make_async_copy(bins_hbm, bins_ref.at[level], sent.at[4]),
        ]
        for c in loads:
            c.start()
        loads[0].wait()
        for q in range(queries):
            qh[q * token_local:(q + 1) * token_local] = qraw[q].astype(F32)
        qb[...] = qh[...].astype(BF)
        loads[1].wait()
        qe[me] = dot(qb[...], proj[...], ((1,), (0,))).astype(BF)
        loads[2].wait()
        pe[0] = dot(ph[...], proj[...], ((1,), (0,))).astype(BF)
        pl.semaphore_wait(barrier, PA + 2 * (half - 1))
        for to in others([0]):
            other_side = jnp.where(to[1] // group == side, 0, 1)
            remote("near", qe.at[me], qe.at[me], device(*to), arrived.at[other_side])
        for k in range(1, half):
            for to in across(k):
                remote("other", pe.at[0], po.at[k - 1, parity], to)
        remote("page", pe.at[0], pe.at[1], partner)
        for k in range(1, half):
            to = across(k)[0]
            remote("click", clicks_hbm, clicks_ref.at[level], to)
            remote("bin", bins_hbm, bins_ref.at[level], to)

        def columns(l, core):
            return pl.ds(pl.multiple_of((2 * l + core) * span, 128), span)

        for l in range(half):
            remote("hidden", ph.at[:, columns(l, 1 - parity)], hx.at[l], partner)
            remote("raw", qb.at[:, columns(l, 1 - parity)], qx.at[l], partner)

        query_of = lax.broadcasted_iota(jnp.int32, (queries, level_tokens), 0)
        token_of = lax.broadcasted_iota(jnp.int32, (queries, level_tokens), 1)
        mask = jnp.where(query_of == lax.rem(token_of, rows) // token_local, 1.0, 0.0)
        for l in range(half):
            pht[l, 0] = ph[:, columns(l, parity)].T
        receive("hidden", hx)
        for l in range(half):
            pht[l, 1] = hx[l].T

        def spread(pages, tok, store):
            top = None
            count = tok.shape[0]
            for k in range(2):
                block = dot(pages(k), tok, ((1,), (1,)))
                lbuf[k, :, :count] = block
                high = jnp.max(block, axis=0, keepdims=True)
                top = high if top is None else jnp.maximum(top, high)
            total = None
            for k in range(2):
                e = jnp.exp2((lbuf[k, :, :count] - top) * FOLDED)
                store(k, e.astype(BF))
                part = jnp.sum(e, axis=0, keepdims=True)
                total = part if total is None else total + part
            return sharpness * top, total

        def lanes_of(start, count):
            return pl.ds(pl.multiple_of(start * rows, 128), count * rows)

        def own_chip(start, count):
            lanes = lanes_of(start, count)

            def store(k, e):
                ebuf[k, :, lanes] = e

            tok = qe[pl.ds(start, count)].reshape(count * rows, E)
            tops[:, lanes], sums[:, lanes] = spread(lambda k: pe[k], tok, store)

        receive("page", pe.at[0])
        receive("near", qe.at[pl.ds(0, group - 1)])
        own_chip(level * PA + group * side, group)
        receive("far", qe.at[pl.ds(0, group)])
        own_chip(level * PA + group * (1 - side), group)
        here = lanes_of(level * PA, PA)
        highs, totals = [tops[:, here]], [sums[:, here]]
        if half > 1:
            receive("other", po)
        for g in range(half - 1):
            def store(k, e):
                eo[g, k] = e

            tok = qe[pl.ds(level * PA, PA)].reshape(level_tokens, E)
            high, total = spread(lambda k: po[g, k], tok, store)
            highs.append(high)
            totals.append(total)
        high = functools.reduce(jnp.maximum, highs)
        total = functools.reduce(jnp.add, [t * jnp.exp(h - high) for h, t in zip(highs, totals)])
        log_norm = high + jnp.log(total)
        norm[me] = log_norm
        for to in others(every):
            remote("norm", norm.at[me], norm.at[me], device(*to))
        for k in range(1, half):
            mine = qe.at[pl.ds(level * PA, PA)]
            remote("level", mine, mine, across(k)[0])

        unit = None
        for g in range(half):
            for k in range(2):
                if g:
                    part = dot(po[g - 1, k], eo[g - 1, k], ((0,), (0,)))
                else:
                    part = dot(pe[k], ebuf[k, :, here], ((0,), (0,)))
                part = part * jnp.exp(highs[g] - log_norm)
                unit = part if unit is None else unit + part
        unit = unit.T.astype(BF)
        for s in range(PA):
            tsend[s] = unit[s * rows:(s + 1) * rows]
        for to_level, to_a in others([0]):
            remote("token", tsend.at[to_a], trecv.at[a], device(to_level, to_a))
        trecv[a] = tsend[a]
        for k in range(2):
            ebt[k, lanes_of(level * PA, PA)] = ebuf[k, :, here].T
        if half > 1:
            receive("level", qe.at[pl.ds(0, (half - 1) * PA)])
        for g in range(1, half):
            start = lax.rem(level + g, half) * PA
            own_chip(start, PA)
            for k in range(2):
                ebt[k, lanes_of(start, PA)] = ebuf[k, :, lanes_of(start, PA)].T
        qt[...] = qe[...].reshape(tokens, E).astype(F32).T

        loads[3].wait()
        loads[4].wait()
        if half > 1:
            receive("click", clicks_ref.at[pl.ds(0, half - 1)])
            receive("bin", bins_ref.at[pl.ds(0, half - 1)])
        pos = [clicks_ref[l, :, 0, :] for l in range(half)]
        neg = [clicks_ref[l, :, 1, :] for l in range(half)]
        weight = [jnp.sqrt(bins_ref[l].astype(F32) + 1.0) for l in range(half)]

        receive("norm", norm.at[pl.ds(0, slots - 1)])
        coeff = []
        for l in range(half):
            rows_in = norm[l * PA:(l + 1) * PA].reshape(PA, level_tokens)
            gap = jnp.zeros(pos[l].shape, F32)
            away = jnp.zeros(pos[l].shape, F32)
            for p in range(PA):
                score = jnp.sum(mask * rows_in[p:p + 1], axis=1, keepdims=True)
                gap = gap + jnp.where(pos[l] == p, score, 0.0)
                away = away + jnp.where(neg[l] == p, score, 0.0)
            coeff.append(-weight[l] * jax.nn.sigmoid(away - gap))

        def score_grad(l, page):
            hits = (pos[l] == page).astype(F32) - (neg[l] == page).astype(F32)
            return jnp.sum(coeff[l] * hits, axis=1, keepdims=True)

        scaled = []
        for l in range(half):
            at = slice(l * level_tokens, (l + 1) * level_tokens)
            factor = jnp.sum(mask * score_grad(l, a), axis=0, keepdims=True)
            factor = factor * jnp.exp(tops[:, at] - norm[l * PA + a])
            scaled.append((qt[:, at] * factor).astype(BF))
        scaled = jnp.concatenate(scaled, axis=1)
        mine = []
        for k in range(2):
            part = dot(scaled, ebt[k], ((1,), (0,)))
            gsend[k] = part.astype(BF)
            remote("patch", gsend.at[k], grecv.at[k], partner)
            mine.append(part)

        column = lax.broadcasted_iota(jnp.int32, (queries, 128), 1)
        table = jnp.zeros((queries, 128), F32)
        for p in range(PA):
            grad = jnp.zeros((queries, 1), F32)
            for l in range(half):
                grad = grad + jnp.where(level == l, score_grad(l, p), 0.0)
            table = jnp.where(column == p, grad, table)
        row_of = lax.broadcasted_iota(jnp.int32, (rows, 128), 0) // token_local
        shares = jnp.zeros((rows, 128), F32)
        for q in range(queries):
            shares = jnp.where(row_of == q, table[q:q + 1], shares)
        receive("token", trecv.at[pl.ds(0, PA - 1)])
        token_own = None
        for p in range(PA):
            part = trecv[p].astype(F32) * shares[:, p:p + 1]
            token_own = part if token_own is None else token_own + part
        token_low = (sharpness * token_own).astype(BF)
        low[0] = token_low
        remote("low", low.at[0], low.at[1], partner)

        receive("raw", qx)
        receive("low", low.at[0])
        for l in range(half):
            wq[l] = dot(qb[:, columns(l, parity)], token_low, ((0,), (0,))) + dot(qx[l], low[1], ((0,), (0,)))

        receive("patch", grecv)
        patch_low = [(sharpness * (mine[k] + grecv[1 - k].astype(F32))).astype(BF).T for k in range(2)]

        for k in every:
            to_level = lax.rem(level + k, half)
            block = wq[to_level]
            for i in range(2):
                block = block + dot(pht[to_level, i], patch_low[i], ((1,), (0,)))
            block = block.astype(BF)
            for s in range(PA):
                wsend[to_level * PA + s] = block[s * chunk:(s + 1) * chunk]
        for to_level, to_a in others(every):
            remote("weight", wsend.at[to_level * PA + to_a], wrecv.at[me], device(to_level, to_a))
        wrecv[me] = wsend[me]

        qgrad = dot(token_low, proj[...], ((1,), (1,)))
        for q in range(queries):
            qg_ref[q] = qgrad[q * token_local:(q + 1) * token_local].astype(BF)
        pg_ref[...] = dot(patch_low[0], proj[...], ((1,), (1,))).astype(BF)

        flush("near", qe.at[pl.ds(0, PA - 1)])
        if half > 1:
            flush("click", clicks_ref.at[pl.ds(0, half - 1)])
            flush("bin", bins_ref.at[pl.ds(0, half - 1)])
            flush("other", po)
            flush("level", qe.at[pl.ds(0, (half - 1) * PA)])
        flush("page", pe.at[0])
        flush("hidden", hx)
        flush("raw", qx)
        flush("norm", norm.at[pl.ds(0, slots - 1)])
        flush("token", tsend.at[pl.ds(0, PA - 1)])
        flush("patch", gsend)
        flush("low", low.at[0])
        flush("weight", wsend.at[pl.ds(0, slots - 1)])
        receive("weight", wrecv.at[pl.ds(0, slots - 1)])
        weight_sum = wrecv[0].astype(F32)
        for s in range(1, slots):
            weight_sum = weight_sum + wrecv[s].astype(F32)
        w_ref[...] = weight_sum

    pl.run_scoped(body, pltpu.SemaphoreType.DMA((LOADS + len(RECEIVED),)))


def writer(qg, pg, w, qg_out, pg_out, w_out, sems):
    copies = [
        pltpu.make_async_copy(pg, pg_out, sems.at[0]),
        pltpu.make_async_copy(qg, qg_out, sems.at[1]),
        pltpu.make_async_copy(w, w_out, sems.at[2]),
    ]
    for c in copies:
        c.start()
    for c in copies:
        c.wait()


def shards(PB, PA, query_hidden, page_hidden, projection, clicks, bins):
    queries, token_local, hidden = query_hidden.shape
    page_count, patches, _ = page_hidden.shape
    assert page_count == 1 and PB % 2 == 0
    E = projection.shape[1]
    rows = queries * token_local
    half = PB // 2
    slots = half * PA
    tokens = rows * slots
    chunk = hidden // (PB * PA)
    span = PA * chunk
    pairs = clicks.shape[1]
    ph = page_hidden.reshape(patches, hidden)
    vmem = pl.BlockSpec(memory_space=pltpu.VMEM)
    hbm = pl.BlockSpec(memory_space=pltpu.HBM)
    dma = lambda n: pltpu.SemaphoreType.DMA((n,))
    outs = (
        jax.ShapeDtypeStruct(query_hidden.shape, BF),
        jax.ShapeDtypeStruct((patches, hidden), BF),
        jax.ShapeDtypeStruct((chunk, E), F32),
    )
    results = pl.pallas_call(
        functools.partial(kernel, PB, PA),
        out_shape=tuple(pltpu.VMEM(o.shape, o.dtype) for o in outs),
        in_specs=[hbm] * 5,
        out_specs=(vmem,) * 3,
        scratch_shapes=[
            pltpu.VMEM((half, queries, 2, pairs), jnp.int32),
            pltpu.VMEM((half, queries, pairs), jnp.int32),
            pltpu.VMEM(query_hidden.shape, BF),
            pltpu.VMEM((rows, hidden), F32),
            pltpu.VMEM((rows, hidden), BF),
            pltpu.VMEM((half, rows, span), BF),
            pltpu.VMEM((patches, hidden), BF),
            pltpu.VMEM((half, patches, span), BF),
            pltpu.VMEM((half, 2, span, patches), BF),
            pltpu.VMEM((hidden, E), BF),
            pltpu.VMEM((slots, rows, E), BF),
            pltpu.VMEM((E, tokens), F32),
            pltpu.VMEM((2, patches, E), BF),
            pltpu.VMEM((max(half - 1, 1), 2, patches, E), BF),
            pltpu.VMEM((2, patches, PA * rows), F32),
            pltpu.VMEM((2, patches, tokens), BF),
            pltpu.VMEM((2, tokens, patches), BF),
            pltpu.VMEM((max(half - 1, 1), 2, patches, PA * rows), BF),
            pltpu.VMEM((1, tokens), F32),
            pltpu.VMEM((1, tokens), F32),
            pltpu.VMEM((slots, 1, PA * rows), F32),
            pltpu.VMEM((PA, rows, E), BF),
            pltpu.VMEM((PA, rows, E), BF),
            pltpu.VMEM((2, E, patches), BF),
            pltpu.VMEM((2, E, patches), BF),
            pltpu.VMEM((2, rows, E), BF),
            pltpu.VMEM((half, span, E), F32),
            pltpu.VMEM((slots, chunk, E), BF),
            pltpu.VMEM((slots, chunk, E), BF),
            dma(len(RECEIVED)),
        ],
        compiler_params=pltpu.CompilerParams(
            collective_id=0, has_side_effects=True, vmem_limit_bytes=65536000
        ),
        name="fused",
    )(query_hidden, ph, projection, jnp.transpose(clicks, (0, 2, 1)), bins)
    query_grad, page_grad, weight_grad = pl.pallas_call(
        writer,
        out_shape=outs,
        in_specs=[vmem] * 3,
        out_specs=(hbm,) * 3,
        scratch_shapes=[dma(3)],
        compiler_params=pltpu.CompilerParams(vmem_limit_bytes=4 * 1024 * 1024),
        name="writer",
    )(*results)
    return query_grad, page_grad.reshape(page_hidden.shape), weight_grad


def solution(mesh):
    return jax.shard_map(
        functools.partial(shards, mesh.shape["pb"], mesh.shape["pa"]),
        mesh=mesh,
        in_specs=(
            P("pb", "pa", None),
            P("pa", "pb", None),
            P(),
            P("pb", None, None),
            P("pb", None),
        ),
        out_specs=(P("pb", "pa", None), P("pa", "pb", None), P(("pb", "pa"), None)),
        check_vma=False,
    )
```

time: 27.8 us -> 25.6 us (0.921)
  the two profiles are of different devices: /device:TPU:0 before, /device:TPU:1 now
where the time goes in v3:
time: 25.6 us; the launch traced here: 25.5 us
  Pallas kernels  24.8 us (97%)
  between operations  0.64 us (2%)
    pallas_call x1, Pallas kernels, shards(): pl.pallas_call(functools.partial(kernel, PB, PA), out_shape=tuple((pltpu....  23.8 us
    pallas_call x1, Pallas kernels, shards(): pl.pallas_call(writer, out_shape=outs, in_specs=[vmem] * 3, out_specs=(hb...  1.03 us

profile of v3, /device:TPU:1, one launch (start us, length us, event | category | flops | bytes accessed | tf_op | source)
XLA Modules:
  0.0 25.5 jit_solution(13151340310134994792)
XLA Ops:
  0.6 23.8 %fused.1 = (bf16[8,4,2048]{2,1,0:T(4,128)(2,1)S(1)}, bf16[256,2048]{1,0:T(8,128)(2,1)S(1)}, f32[64,128]{1,0:T(8,128)S(1)}) custom-call(bf16[8,4,2048]{2,1,0:T(4,128)(2,1)} %qh_hbm.1, bf16[256,2048]{1,0:T(8,128)(2,1)} %bitcast.3, bf16[2048,128]{1,0:T(8,128)(2,1)} %proj_hbm.1, s32[8,2,8]{2,1,0:T(2,128)} %bitcast.4, s32[8,8]{1,0:T(8,128)} %bins_hbm.1), custom_call_target="tpu_custom_call" | custom-call | tf_op jit(solution)/shard_map/fused/pallas_call | solution.py:369
  24.4 1.0 %writer.1 = (bf16[8,4,2048]{2,1,0:T(4,128)(2,1)}, bf16[256,2048]{1,0:T(8,128)(2,1)}, f32[64,128]{1,0:T(8,128)}) custom-call(bf16[8,4,2048]{2,1,0:T(4,128)(2,1)S(1)} %get-tuple-element.9.qg, bf16[256,2048]{1,0:T(8,128)(2,1)S(1)} %get-tuple-element.10.pg, f32[64,128]{1,0:T(8,128)S(1)} %get-tuple-element.11.w), custom_call_target="tpu_custom_call" | custom-call | tf_op jit(solution)/shard_map/writer/pallas_call | solution.py:411

commit v4 on v3

--- a/solution.py
+++ b/solution.py
@@ -26,7 +26,7 @@
 def kernel(
     PB, PA, qh_hbm, ph_hbm, proj_hbm, clicks_hbm, bins_hbm,
     qg_ref, pg_ref, w_ref,
-    clicks_ref, bins_ref, qraw, qh, qb, qx, ph, hx, pht, proj, qe, qt, pe, po, lbuf, ebuf, ebt, eo, tops, sums, norm,
+    clicks_ref, bins_ref, qraw, qh, qb, qx, qt2, ph, hx, pht, proj, qe, qt, pe, po, lbuf, ebuf, ebt, eo, tops, sums, norm,
     tsend, trecv, gsend, grecv, low, wq, wsend, wrecv, arrived,
 ):
     b = lax.axis_index("pb")
@@ -53,9 +53,9 @@
     group = PA // 2
     side = a // group
 
-    def others(offsets):
+    def others(offsets, ascending=False):
         for i in range(deep):
-            far = jnp.where(upper, i, deep - 1 - i)
+            far = i if ascending else jnp.where(upper, i, deep - 1 - i)
             for k in offsets:
                 to_level = lax.rem(level + k, half)
                 for j in list(range(1, width)) + [0]:
@@ -65,7 +65,7 @@
                             continue
                         up = i + jnp.where(i >= z, 1, 0)
                         down = deep - 1 - i - jnp.where(deep - 1 - i <= z, 1, 0)
-                        to_z = jnp.where(upper, up, down)
+                        to_z = up if ascending else jnp.where(upper, up, down)
                     yield to_level, to_z * width + lax.rem(x + j, width)
 
     every = list(range(1, half)) + [0]
@@ -117,12 +117,12 @@
         loads[2].wait()
         pe[0] = dot(ph[...], proj[...], ((1,), (0,))).astype(BF)
         pl.semaphore_wait(barrier, PA + 2 * (half - 1))
+        for k in range(1, half):
+            for to in across(k):
+                remote("other", pe.at[0], po.at[k - 1, parity], to)
         for to in others([0]):
             other_side = jnp.where(to[1] // group == side, 0, 1)
             remote("near", qe.at[me], qe.at[me], device(*to), arrived.at[other_side])
-        for k in range(1, half):
-            for to in across(k):
-                remote("other", pe.at[0], po.at[k - 1, parity], to)
         remote("page", pe.at[0], pe.at[1], partner)
         for k in range(1, half):
             to = across(k)[0]
@@ -144,6 +144,10 @@
         receive("hidden", hx)
         for l in range(half):
             pht[l, 1] = hx[l].T
+        receive("raw", qx)
+        for l in range(half):
+            qt2[l, :, :rows] = qb[:, columns(l, parity)].T
+            qt2[l, :, rows:] = qx[l].T
 
         def spread(pages, tok, store):
             top = None
@@ -285,10 +289,9 @@
         low[0] = token_low
         remote("low", low.at[0], low.at[1], partner)
 
-        receive("raw", qx)
         receive("low", low.at[0])
         for l in range(half):
-            wq[l] = dot(qb[:, columns(l, parity)], token_low, ((0,), (0,))) + dot(qx[l], low[1], ((0,), (0,)))
+            wq[l] = dot(qt2[l], low[...].reshape(2 * rows, E), ((1,), (0,)))
 
         receive("patch", grecv)
         patch_low = [(sharpness * (mine[k] + grecv[1 - k].astype(F32))).astype(BF).T for k in range(2)]
@@ -301,7 +304,10 @@
             block = block.astype(BF)
             for s in range(PA):
                 wsend[to_level * PA + s] = block[s * chunk:(s + 1) * chunk]
-        for to_level, to_a in others(every):
+        place = a * half + level
+        for n in range(slots - 1):
+            d = n + jnp.where(n >= place, 1, 0)
+            to_level, to_a = lax.rem(d, half), d // half
             remote("weight", wsend.at[to_level * PA + to_a], wrecv.at[me], device(to_level, to_a))
         wrecv[me] = wsend[me]
 
@@ -378,6 +384,7 @@
             pltpu.VMEM((rows, hidden), F32),
             pltpu.VMEM((rows, hidden), BF),
             pltpu.VMEM((half, rows, span), BF),
+            pltpu.VMEM((half, span, 2 * rows), BF),
             pltpu.VMEM((patches, hidden), BF),
             pltpu.VMEM((half, patches, span), BF),
             pltpu.VMEM((half, 2, span, patches), BF),

time: 25.6 us -> 24.7 us (0.965)
  the two profiles are of different devices: /device:TPU:1 before, /device:TPU:0 now
where the time goes in v4:
time: 24.7 us; the launch traced here: 24.3 us
  Pallas kernels  23.7 us (96%)
  between operations  0.64 us (3%)
    pallas_call x1, Pallas kernels, shards(): pl.pallas_call(functools.partial(kernel, PB, PA), out_shape=tuple((pltpu....  22.7 us
    pallas_call x1, Pallas kernels, shards(): pl.pallas_call(writer, out_shape=outs, in_specs=[vmem] * 3, out_specs=(hb...  1.03 us

profile of v4, /device:TPU:0, one launch (start us, length us, event | category | flops | bytes accessed | tf_op | source)
XLA Modules:
  0.0 24.3 jit_solution(3483015398379337548)
XLA Ops:
  0.6 22.7 %fused.1 = (bf16[8,4,2048]{2,1,0:T(4,128)(2,1)S(1)}, bf16[256,2048]{1,0:T(8,128)(2,1)S(1)}, f32[64,128]{1,0:T(8,128)S(1)}) custom-call(bf16[8,4,2048]{2,1,0:T(4,128)(2,1)} %qh_hbm.1, bf16[256,2048]{1,0:T(8,128)(2,1)} %bitcast.3, bf16[2048,128]{1,0:T(8,128)(2,1)} %proj_hbm.1, s32[8,2,8]{2,1,0:T(2,128)} %bitcast.4, s32[8,8]{1,0:T(8,128)} %bins_hbm.1), custom_call_target="tpu_custom_call" | custom-call | tf_op jit(solution)/shard_map/fused/pallas_call | solution.py:375
  23.3 1.0 %writer.1 = (bf16[8,4,2048]{2,1,0:T(4,128)(2,1)}, bf16[256,2048]{1,0:T(8,128)(2,1)}, f32[64,128]{1,0:T(8,128)}) custom-call(bf16[8,4,2048]{2,1,0:T(4,128)(2,1)S(1)} %get-tuple-element.9.qg, bf16[256,2048]{1,0:T(8,128)(2,1)S(1)} %get-tuple-element.10.pg, f32[64,128]{1,0:T(8,128)S(1)} %get-tuple-element.11.w), custom_call_target="tpu_custom_call" | custom-call | tf_op jit(solution)/shard_map/writer/pallas_call | solution.py:418

commit v5 on v4

--- a/solution.py
+++ b/solution.py
@@ -178,10 +178,13 @@
             tops[:, lanes], sums[:, lanes] = spread(lambda k: pe[k], tok, store)
 
         receive("page", pe.at[0])
-        receive("near", qe.at[pl.ds(0, group - 1)])
-        own_chip(level * PA + group * side, group)
-        receive("far", qe.at[pl.ds(0, group)])
-        own_chip(level * PA + group * (1 - side), group)
+        for kind, part in (("near", side), ("far", 1 - side)):
+            start = level * PA + group * part
+            receive(kind, qe.at[pl.ds(0, group - 1 if kind == "near" else group)])
+            for k in range(1, half):
+                batch = qe.at[pl.ds(start, group)]
+                remote("level", batch, batch, across(k)[0])
+            own_chip(start, group)
         here = lanes_of(level * PA, PA)
         highs, totals = [tops[:, here]], [sums[:, here]]
         if half > 1:
@@ -200,9 +203,6 @@
         norm[me] = log_norm
         for to in others(every):
             remote("norm", norm.at[me], norm.at[me], device(*to))
-        for k in range(1, half):
-            mine = qe.at[pl.ds(level * PA, PA)]
-            remote("level", mine, mine, across(k)[0])
 
         unit = None
         for g in range(half):

time: 24.7 us -> 24.8 us (level)
  the two profiles are of different devices: /device:TPU:0 before, /device:TPU:11 now
where the time goes in v5:
time: 24.8 us; the launch traced here: 24.6 us
  Pallas kernels  24 us (97%)
  between operations  0.64 us (3%)
    pallas_call x1, Pallas kernels, shards(): pl.pallas_call(functools.partial(kernel, PB, PA), out_shape=tuple((pltpu....  22.9 us
    pallas_call x1, Pallas kernels, shards(): pl.pallas_call(writer, out_shape=outs, in_specs=[vmem] * 3, out_specs=(hb...  1.03 us

profile of v5, /device:TPU:11, one launch (start us, length us, event | category | flops | bytes accessed | tf_op | source)
XLA Modules:
  0.0 24.6 jit_solution(18057487763206914361)
XLA Ops:
  0.6 22.9 %fused.1 = (bf16[8,4,2048]{2,1,0:T(4,128)(2,1)S(1)}, bf16[256,2048]{1,0:T(8,128)(2,1)S(1)}, f32[64,128]{1,0:T(8,128)S(1)}) custom-call(bf16[8,4,2048]{2,1,0:T(4,128)(2,1)} %qh_hbm.1, bf16[256,2048]{1,0:T(8,128)(2,1)} %bitcast.3, bf16[2048,128]{1,0:T(8,128)(2,1)} %proj_hbm.1, s32[8,2,8]{2,1,0:T(2,128)} %bitcast.4, s32[8,8]{1,0:T(8,128)} %bins_hbm.1), custom_call_target="tpu_custom_call" | custom-call | tf_op jit(solution)/shard_map/fused/pallas_call | solution.py:375
  23.6 1.0 %writer.1 = (bf16[8,4,2048]{2,1,0:T(4,128)(2,1)}, bf16[256,2048]{1,0:T(8,128)(2,1)}, f32[64,128]{1,0:T(8,128)}) custom-call(bf16[8,4,2048]{2,1,0:T(4,128)(2,1)S(1)} %get-tuple-element.9.qg, bf16[256,2048]{1,0:T(8,128)(2,1)S(1)} %get-tuple-element.10.pg, f32[64,128]{1,0:T(8,128)S(1)} %get-tuple-element.11.w), custom_call_target="tpu_custom_call" | custom-call | tf_op jit(solution)/shard_map/writer/pallas_call | solution.py:418
